TPU v7x, 32 devices: a whole 2x2x4 slice. The times are simulated.
32 devices in a mesh: blk: 4 (over x, core), uly: 8 (over z, y).
Axes of the slice: x: 2, y: 2, z: 4, core: 2. Of those that a mesh axis runs over, the one named last changes fastest.
Arguments:
- query: bfloat16 [4096, 4096], P(('blk', 'uly')), may hold values from -5 to 5
- key_input: bfloat16 [4096, 512], P(('blk', 'uly')), may hold values from -5 to 5
- value_input: bfloat16 [4096, 512], P(('blk', 'uly')), may hold values from -6 to 6
- output: bfloat16 [4096, 4096], P(('blk', 'uly')), may hold values from -6 to 6
- out_grad: bfloat16 [4096, 4096], P(('blk', 'uly')), may hold values from -6 to 6
Outputs:
- query_grad: bfloat16 [4096, 4096], P(('blk', 'uly'))
- key_gradient: bfloat16 [4096, 512], P(('blk', 'uly'))
- value_gradient: bfloat16 [4096, 512], P(('blk', 'uly'))
All inputs are finite; a program needn't handle non-finite values.
Results may differ from a plain program's by a relative error of at most 0.009.
Values may be sent and summed in bfloat16 or wider, within the bound.
A program may use at most 64 MiB of HBM per device.

v0:
```python
import jax
import jax.numpy as jnp
from jax import lax
from jax.sharding import PartitionSpec as P

QUERY_HEADS = 32
KEY_VALUE_HEADS = 4
HEAD_SIZE = 128
WINDOW_KEYS = 1024


def shifted(value, axis, steps):
    count = lax.axis_size(axis)
    leading, last = (max(0, -steps), min(count, count - steps))
    return lax.ppermute(value, axis, [(source, source + steps) for source in range(leading, last)])


def local(query, key_input, value_input, output, out_grad):
    token_rows = query.shape[0]
    ulysses_count = lax.axis_size("uly")
    local_heads = QUERY_HEADS // ulysses_count
    group_extent = ulysses_count // KEY_VALUE_HEADS
    scaling = HEAD_SIZE ** (-0.5)
    rows_here = token_rows * ulysses_count
    block = min(512, rows_here)
    span = WINDOW_KEYS + block
    block_count = rows_here // block
    own_dot = jnp.sum(
        output.reshape(token_rows, QUERY_HEADS, HEAD_SIZE).astype(jnp.float32)
        * out_grad.reshape(token_rows, QUERY_HEADS, HEAD_SIZE).astype(jnp.float32),
        axis=2,
    )
    query_here, grad_here = (
        lax.all_to_all(query, "uly", split_axis=1, concat_axis=0, tiled=True),
        lax.all_to_all(out_grad, "uly", split_axis=1, concat_axis=0, tiled=True),
    )
    row_dot = lax.all_to_all(own_dot, "uly", split_axis=1, concat_axis=0, tiled=True)

    def repeat_groups(value_entries):
        return jnp.repeat(
            value_entries.reshape(token_rows, KEY_VALUE_HEADS, HEAD_SIZE), group_extent, axis=1
        ).reshape(token_rows, ulysses_count * HEAD_SIZE)

    key_head, value_head = (
        lax.all_to_all(repeat_groups(key_input), "uly", split_axis=1, concat_axis=0, tiled=True),
        lax.all_to_all(repeat_groups(value_input), "uly", split_axis=1, concat_axis=0, tiled=True),
    )
    queries = query_here.reshape(rows_here, local_heads, HEAD_SIZE)
    grads_out = grad_here.reshape(rows_here, local_heads, HEAD_SIZE)
    tail_keys, tail_values = shifted(
        (key_head[rows_here - WINDOW_KEYS :], value_head[rows_here - WINDOW_KEYS :]), "blk", 1
    )
    key_ext = jnp.concatenate([tail_keys, key_head], axis=0)
    value_ext = jnp.concatenate([tail_values, value_head], axis=0)
    block_anchor = lax.axis_index("blk") * rows_here - WINDOW_KEYS
    offsets = jnp.arange(block, dtype=jnp.int32)[:, None]
    columns = jnp.arange(span, dtype=jnp.int32)[None, :]
    relative = columns - offsets
    inside = (relative >= 1) & (relative <= WINDOW_KEYS)

    def block_step(index, carry):
        query_acc, key_acc, value_acc = carry
        start = index * block
        query_block = lax.dynamic_slice_in_dim(queries, start, block, 0)
        grad_block = lax.dynamic_slice_in_dim(grads_out, start, block, 0)
        dot_block = lax.dynamic_slice_in_dim(row_dot, start, block, 0)
        key_block = lax.dynamic_slice_in_dim(key_ext, start, span, 0)
        value_block = lax.dynamic_slice_in_dim(value_ext, start, span, 0)
        visible = (inside & (block_anchor + start + columns >= 0))[None, :, :]
        scores = (
            jnp.einsum("qhd,kd->hqk", query_block, key_block, preferred_element_type=jnp.float32)
            * scaling
        )
        masked = jnp.where(visible, scores, -1e30)
        row_max = jnp.max(masked, axis=2)
        row_sum = jnp.sum(jnp.where(visible, jnp.exp(masked - row_max[:, :, None]), 0.0), axis=2)
        log_total = row_max + jnp.log(row_sum)
        weights = jnp.where(visible, jnp.exp(masked - log_total[:, :, None]), 0.0)
        weights_low = weights.astype(jnp.bfloat16)
        weight_grad = jnp.einsum(
            "qhd,kd->hqk", grad_block, value_block, preferred_element_type=jnp.float32
        )
        score_grad = (weights * (weight_grad - dot_block.T[:, :, None]) * scaling).astype(
            jnp.bfloat16
        )
        query_portion = jnp.einsum(
            "hqk,kd->qhd", score_grad, key_block, preferred_element_type=jnp.float32
        )
        key_portion = jnp.einsum(
            "hqk,qhd->kd", score_grad, query_block, preferred_element_type=jnp.float32
        )
        value_portion = jnp.einsum(
            "hqk,qhd->kd", weights_low, grad_block, preferred_element_type=jnp.float32
        )
        query_acc = lax.dynamic_update_slice_in_dim(query_acc, query_portion, start, 0)
        key_acc = lax.dynamic_update_slice_in_dim(
            key_acc, lax.dynamic_slice_in_dim(key_acc, start, span, 0) + key_portion, start, 0
        )
        value_acc = lax.dynamic_update_slice_in_dim(
            value_acc, lax.dynamic_slice_in_dim(value_acc, start, span, 0) + value_portion, start, 0
        )
        return (query_acc, key_acc, value_acc)

    grad_init = (
        jnp.zeros((rows_here, local_heads, HEAD_SIZE), jnp.float32),
        jnp.zeros((WINDOW_KEYS + rows_here, HEAD_SIZE), jnp.float32),
        jnp.zeros((WINDOW_KEYS + rows_here, HEAD_SIZE), jnp.float32),
    )
    query_acc, key_acc, value_acc = lax.fori_loop(0, block_count, block_step, grad_init)
    tail_key, tail_value = (
        shifted(key_acc[:WINDOW_KEYS].astype(jnp.bfloat16), "blk", -1).astype(jnp.float32),
        shifted(value_acc[:WINDOW_KEYS].astype(jnp.bfloat16), "blk", -1).astype(jnp.float32),
    )
    key_own = jnp.concatenate(
        [key_acc[WINDOW_KEYS:rows_here], key_acc[rows_here:] + tail_key], axis=0
    )
    value_own = jnp.concatenate(
        [value_acc[WINDOW_KEYS:rows_here], value_acc[rows_here:] + tail_value], axis=0
    )
    query_low = query_acc.astype(jnp.bfloat16).reshape(rows_here, local_heads * HEAD_SIZE)
    query_grad = lax.all_to_all(query_low, "uly", split_axis=0, concat_axis=1, tiled=True)
    key_portions, value_portions = (
        lax.all_to_all(
            key_own.reshape(ulysses_count, token_rows, HEAD_SIZE).astype(jnp.bfloat16),
            "uly",
            split_axis=0,
            concat_axis=0,
            tiled=True,
        ).astype(jnp.float32),
        lax.all_to_all(
            value_own.reshape(ulysses_count, token_rows, HEAD_SIZE).astype(jnp.bfloat16),
            "uly",
            split_axis=0,
            concat_axis=0,
            tiled=True,
        ).astype(jnp.float32),
    )
    key_totals = key_portions.reshape(KEY_VALUE_HEADS, group_extent, token_rows, HEAD_SIZE).sum(
        axis=1
    )
    value_totals = value_portions.reshape(KEY_VALUE_HEADS, group_extent, token_rows, HEAD_SIZE).sum(
        axis=1
    )
    key_gradient = (
        key_totals.transpose(1, 0, 2)
        .reshape(token_rows, KEY_VALUE_HEADS * HEAD_SIZE)
        .astype(jnp.bfloat16)
    )
    value_gradient = (
        value_totals.transpose(1, 0, 2)
        .reshape(token_rows, KEY_VALUE_HEADS * HEAD_SIZE)
        .astype(jnp.bfloat16)
    )
    return (query_grad, key_gradient, value_gradient)


def solution(mesh):
    in_specs = (
        P(("blk", "uly"), None),
        P(("blk", "uly"), None),
        P(("blk", "uly"), None),
        P(("blk", "uly"), None),
        P(("blk", "uly"), None),
    )
    out_specs = (P(("blk", "uly"), None), P(("blk", "uly"), None), P(("blk", "uly"), None))
    return jax.shard_map(local, mesh=mesh, in_specs=in_specs, out_specs=out_specs, check_vma=False)
```

profile of v0, /device:TPU:0, one launch (start us, length us, event | category | flops | bytes accessed | tf_op | source)
XLA Modules:
  0.0 205.3 jit_solution(4544083041959012274)
XLA Ops:
  0.6 0.9 copy-done
  1.6 0.7 broadcast_in_dim.64
  2.3 7.3 %all-to-all-start = ((bf16[128,8,128]{2,0,1:T(8,128)(2,1)}), bf16[128,8,128]{2,0,1:T(8,128)(2,1)S(1)}, u32[]{:S(2)}, u32[]{:S(2)}) async-start(bf16[128,8,128]{2,0,1:T(8,128)(2,1)} %bitcast), calls=%async_computation | async-start | bytes 524288 | tf_op jit(solution)/shard_map/all_to_all | solution.py:45
  9.6 0.9 copy_bitcast_fusion
  10.5 8.0 %all-to-all-done = bf16[128,8,128]{2,0,1:T(8,128)(2,1)S(1)} async-done(((bf16[128,8,128]{2,0,1:T(8,128)(2,1)}), bf16[128,8,128]{2,0,1:T(8,128)(2,1)S(1)}, u32[]{:S(2)}, u32[]{:S(2)}) %all-to-all-start) | async-done | bytes 262176 | tf_op jit(solution)/shard_map/all_to_all | solution.py:45
  18.5 0.7 broadcast_in_dim.65
  19.3 4.0 %all-to-all-start.2 = ((bf16[128,8,128]{2,0,1:T(8,128)(2,1)}), bf16[128,8,128]{2,0,1:T(8,128)(2,1)}, u32[]{:S(2)}, u32[]{:S(2)}) async-start(bf16[128,8,128]{2,0,1:T(8,128)(2,1)} %bitcast.5), calls=%async_computation.2 | async-start | bytes 524288 | tf_op jit(solution)/shard_map/all_to_all | solution.py:46
  23.3 2.3 %copy.37 = bf16[128,4096]{0,1:T(8,128)(2,1)} copy(bf16[128,4096]{1,0:T(8,128)(2,1)} %param.7) | data formatting | bytes 2097152 | tf_op args[0]
  25.6 6.1 %all-to-all-done.2 = bf16[128,8,128]{2,0,1:T(8,128)(2,1)} async-done(((bf16[128,8,128]{2,0,1:T(8,128)(2,1)}), bf16[128,8,128]{2,0,1:T(8,128)(2,1)}, u32[]{:S(2)}, u32[]{:S(2)}) %all-to-all-start.2) | async-done | bytes 262176 | tf_op jit(solution)/shard_map/all_to_all | solution.py:46
  31.7 3.6 %all-to-all-start.1 = ((bf16[128,8,512]{0,2,1:T(8,128)(2,1)}), bf16[128,8,512]{0,2,1:T(8,128)(2,1)S(1)}, u32[]{:S(2)}, u32[]{:S(2)}) async-start(bf16[128,8,512]{0,2,1:T(8,128)(2,1)} %bitcast.3), calls=%async_computation.1 | async-start | bytes 2097152 | tf_op jit(solution)/shard_map/all_to_all | solution.py:34
  35.2 2.3 %copy.40 = bf16[128,4096]{0,1:T(8,128)(2,1)} copy(bf16[128,4096]{1,0:T(8,128)(2,1)} %param.11) | data formatting | bytes 2097152 | tf_op args[4]
  37.5 23.2 %all-to-all-done.1 = bf16[128,8,512]{0,2,1:T(8,128)(2,1)S(1)} async-done(((bf16[128,8,512]{0,2,1:T(8,128)(2,1)}), bf16[128,8,512]{0,2,1:T(8,128)(2,1)S(1)}, u32[]{:S(2)}, u32[]{:S(2)}) %all-to-all-start.1) | async-done | bytes 1048608 | tf_op jit(solution)/shard_map/all_to_all | solution.py:34
  60.7 4.2 %all-to-all-start.3 = ((bf16[128,8,512]{0,2,1:T(8,128)(2,1)}), bf16[128,8,512]{0,2,1:T(8,128)(2,1)}, u32[]{:S(2)}, u32[]{:S(2)}) async-start(bf16[128,8,512]{0,2,1:T(8,128)(2,1)} %bitcast.8), calls=%async_computation.3 | async-start | bytes 2097152 | tf_op jit(solution)/shard_map/all_to_all | solution.py:35
  64.9 2.0 collective-permute-start.1
  67.0 4.1 %collective-permute-start = (bf16[1024,128]{1,0:T(8,128)(2,1)S(1)}, bf16[1024,128]{1,0:T(8,128)(2,1)}, u32[]{:S(2)}, u32[]{:S(2)}) collective-permute-start(bf16[1024,128]{1,0:T(8,128)(2,1)S(1)} %bitcast.139), channel_id=1, source_target_pairs={{0,8},{8,16},{16,24},{1,9},{9,17},{17,25},{2,10},{10,18},{18,26},{... | collective-permute-start | bytes 786440 | tf_op jit(solution)/shard_map/ppermute | solution.py:15
  71.1 1.8 multiply_bitcast_fusion
  72.9 1.7 copy.60
  74.6 2.2 %reduce_sum.40 = f32[128,32]{1,0:T(8,128)S(1)} reduce(f32[128,32,128]{2,1,0:T(8,128)} %bitcast.135, f32[]{:T(128)} %constant.72.clone.1), dimensions={2}, to_apply=%region_0.0 | reduce | flops 520192 | bytes 2113540 | tf_op jit(solution)/shard_map/reduce_sum | solution.py:28
  76.8 0.7 copy.42
  77.5 1.9 pad_maximum_fusion.1
  79.3 11.0 %all-to-all-done.3 = bf16[128,8,512]{0,2,1:T(8,128)(2,1)} async-done(((bf16[128,8,512]{0,2,1:T(8,128)(2,1)}), bf16[128,8,512]{0,2,1:T(8,128)(2,1)}, u32[]{:S(2)}, u32[]{:S(2)}) %all-to-all-start.3) | async-done | bytes 1048608 | tf_op jit(solution)/shard_map/all_to_all | solution.py:35
  90.3 3.4 %all-to-all-start.4 = ((f32[128,8,4]{0,2,1:T(4,128)}), f32[128,8,4]{0,2,1:T(4,128)S(1)}, u32[]{:S(2)}, u32[]{:S(2)}) async-start(f32[128,8,4]{0,2,1:T(4,128)} %bitcast.10), calls=%async_computation.4 | async-start | bytes 32768 | tf_op jit(solution)/shard_map/all_to_all | solution.py:37
  93.7 1.0 pad_maximum_fusion
  94.7 0.7 copy.38
  95.4 0.5 reshape.112
  95.9 1.9 copy.41
  97.8 1.3 reshape.114
  99.1 1.2 all-to-all-done.4
  100.3 1.1 broadcast.52.clone
  101.4 1.1 broadcast_in_dim.63
  102.5 39.7 %while.18 = (s32[]{:T(128)}, bf16[1024,4,128]{0,2,1:T(8,128)(2,1)}, f32[2048,128]{1,0:T(8,128)S(1)}, f32[2048,128]{1,0:T(8,128)}, bf16[2048,128]{1,0:T(8,128)(2,...) while((s32[]{:T(128)}, bf16[1024,4,128]{0,2,1:T(8,128)(2,1)}, ...), condition=%wide.region_4.5_spmd.clone, body=%wide.region_1.4_spmd.clone.sunk | while | flops 4096918528 | bytes 95382904 | solution.py:109
  102.6 1.4 fusion.73
  104.0 2.4 %fusion.74 = (f32[4,512]{1,0:T(4,128)S(1)}, f32[1536,512,4]{1,0,2:T(8,128)S(1)}) fusion(pred[512,1536]{0,1:T(8,128)(4,1)S(1)} %fusion.73, bf16[1024,4,128]{0,2,1:T(8,128)(2,1)S(1)} %get-tuple-element.386, s32[]{:T(128)S(6)} %select_n.94, bf16[2048,128]{1,0:T(8,128)(2,1)S(1)} %get-tuple-element.384, s32[]{:T(128)S(6)} %select_n.95), kind=kOutput, calls=%fused_computation.10.clone.1 | convolution fusion | flops 814741504 | bytes 14295048 | tf_op jit(solution)/shard_map/while/body/eval_jaxpr/qhd,kd->hqk/dot_general | solution.py:71
  106.3 3.1 %select_reduce_fusion.2 = f32[4,512]{1,0:T(4,128)S(1)} fusion(f32[1536,512,4]{1,0,2:T(8,128)S(1)} %get-tuple-element.348, f32[4,512]{1,0:T(4,128)S(1)} %get-tuple-element.349, pred[512,1536]{0,1:T(8,128)(4,1)S(1)} %fusion.73), kind=kLoop, calls=%fused_computation.8.clone.1 | loop fusion | flops 15726592 | bytes 13385728 | tf_op jit(solution)/shard_map/while/body/eval_jaxpr/reduce_sum | solution.py:76
  109.5 4.1 %fusion.78 = f32[2048,128]{1,0:T(8,128)S(1)} fusion(f32[2048,128]{1,0:T(8,128)S(1)} %copy-done.1, s32[]{:T(128)S(6)} %select_n.95, f32[1536,512,4]{1,0,2:T(8,128)S(1)} %get-tuple-element.348, f32[4,512]{1,0:T(4,128)S(1)} %log_add_fusion.2, pred[512,1536]{0,1:T(8,128)(4,1)S(1)} %fusion.73, bf16[1024,4,128]{0,2,1:T(8,128)(2,1)S(1)} %copy-done.3, ...), kind=kOutput, calls=%fused_computation.20.clone.1 | convolution fusion | flops 821231616 | bytes 15474696 | tf_op jit(solution)/shard_map/while/body/eval_jaxpr/hqk,qhd->kd/dot_general | solution.py:92
  113.6 5.1 %fusion.75 = bf16[4,512,1536]{1,2,0:T(8,128)(2,1)S(1)} fusion(f32[1536,512,4]{1,0,2:T(8,128)S(1)} %get-tuple-element.348, f32[4,512]{1,0:T(4,128)S(1)} %dynamic-slice_bitcast_fusion.2, f32[4,512]{1,0:T(4,128)S(1)} %log_add_fusion.2, pred[512,1536]{0,1:T(8,128)(4,1)S(1)} %fusion.73, bf16[1024,4,128]{0,2,1:T(8,128)(2,1)S(1)} %copy-done.3, ...), kind=kOutput, calls=%fused_computation.5.clone.1 | convolution fusion | flops 830472192 | bytes 20594696 | tf_op jit(solution)/shard_map/while/body/eval_jaxpr/qhd,kd->hqk/dot_general | solution.py:80
  118.7 1.8 fusion.77
  120.5 1.8 fusion.76
  122.4 1.4 fusion.73
  123.8 2.4 %fusion.74 = (f32[4,512]{1,0:T(4,128)S(1)}, f32[1536,512,4]{1,0,2:T(8,128)S(1)}) fusion(pred[512,1536]{0,1:T(8,128)(4,1)S(1)} %fusion.73, bf16[1024,4,128]{0,2,1:T(8,128)(2,1)S(1)} %get-tuple-element.386, s32[]{:T(128)S(6)} %select_n.94, bf16[2048,128]{1,0:T(8,128)(2,1)S(1)} %get-tuple-element.384, s32[]{:T(128)S(6)} %select_n.95), kind=kOutput, calls=%fused_computation.10.clone.1 | convolution fusion | flops 814741504 | bytes 14295048 | tf_op jit(solution)/shard_map/while/body/eval_jaxpr/qhd,kd->hqk/dot_general | solution.py:71
  126.2 3.1 %select_reduce_fusion.2 = f32[4,512]{1,0:T(4,128)S(1)} fusion(f32[1536,512,4]{1,0,2:T(8,128)S(1)} %get-tuple-element.348, f32[4,512]{1,0:T(4,128)S(1)} %get-tuple-element.349, pred[512,1536]{0,1:T(8,128)(4,1)S(1)} %fusion.73), kind=kLoop, calls=%fused_computation.8.clone.1 | loop fusion | flops 15726592 | bytes 13385728 | tf_op jit(solution)/shard_map/while/body/eval_jaxpr/reduce_sum | solution.py:76
  129.4 4.1 %fusion.78 = f32[2048,128]{1,0:T(8,128)S(1)} fusion(f32[2048,128]{1,0:T(8,128)S(1)} %copy-done.1, s32[]{:T(128)S(6)} %select_n.95, f32[1536,512,4]{1,0,2:T(8,128)S(1)} %get-tuple-element.348, f32[4,512]{1,0:T(4,128)S(1)} %log_add_fusion.2, pred[512,1536]{0,1:T(8,128)(4,1)S(1)} %fusion.73, bf16[1024,4,128]{0,2,1:T(8,128)(2,1)S(1)} %copy-done.3, ...), kind=kOutput, calls=%fused_computation.20.clone.1 | convolution fusion | flops 821231616 | bytes 15474696 | tf_op jit(solution)/shard_map/while/body/eval_jaxpr/hqk,qhd->kd/dot_general | solution.py:92
  133.5 5.1 %fusion.75 = bf16[4,512,1536]{1,2,0:T(8,128)(2,1)S(1)} fusion(f32[1536,512,4]{1,0,2:T(8,128)S(1)} %get-tuple-element.348, f32[4,512]{1,0:T(4,128)S(1)} %dynamic-slice_bitcast_fusion.2, f32[4,512]{1,0:T(4,128)S(1)} %log_add_fusion.2, pred[512,1536]{0,1:T(8,128)(4,1)S(1)} %fusion.73, bf16[1024,4,128]{0,2,1:T(8,128)(2,1)S(1)} %copy-done.3, ...), kind=kOutput, calls=%fused_computation.5.clone.1 | convolution fusion | flops 830472192 | bytes 20594696 | tf_op jit(solution)/shard_map/while/body/eval_jaxpr/qhd,kd->hqk/dot_general | solution.py:80
  138.6 1.8 fusion.77
  140.4 1.8 fusion.76
  142.3 1.3 collective-permute-start.2
  143.6 1.1 slice.24
  144.6 1.3 collective-permute-start.3
  146.0 0.8 add_convert_fusion.1
  146.7 4.8 %all-to-all-start.6 = ((bf16[8,128,128]{2,1,0:T(8,128)(2,1)}), bf16[8,128,128]{2,1,0:T(8,128)(2,1)S(1)}, u32[]{:S(2)}, u32[]{:S(2)}) async-start(bf16[8,128,128]{2,1,0:T(8,128)(2,1)} %bitcast.15), calls=%async_computation.6 | async-start | bytes 524288 | tf_op jit(solution)/shard_map/all_to_all | solution.py:123
  151.5 1.8 add_convert_fusion
  153.3 6.4 %all-to-all-done.6 = bf16[8,128,128]{2,1,0:T(8,128)(2,1)S(1)} async-done(((bf16[8,128,128]{2,1,0:T(8,128)(2,1)}), bf16[8,128,128]{2,1,0:T(8,128)(2,1)S(1)}, u32[]{:S(2)}, u32[]{:S(2)}) %all-to-all-start.6) | async-done | bytes 262176 | tf_op jit(solution)/shard_map/all_to_all | solution.py:123
  159.7 3.8 %all-to-all-start.7 = ((bf16[8,128,128]{2,1,0:T(8,128)(2,1)}), bf16[8,128,128]{2,1,0:T(8,128)(2,1)S(1)}, u32[]{:S(2)}, u32[]{:S(2)}) async-start(bf16[8,128,128]{2,1,0:T(8,128)(2,1)} %bitcast.19), calls=%async_computation.7 | async-start | bytes 524288 | tf_op jit(solution)/shard_map/all_to_all | solution.py:130
  163.5 1.5 copy.61
  165.0 1.5 copy.54
  166.4 6.0 %all-to-all-done.7 = bf16[8,128,128]{2,1,0:T(8,128)(2,1)S(1)} async-done(((bf16[8,128,128]{2,1,0:T(8,128)(2,1)}), bf16[8,128,128]{2,1,0:T(8,128)(2,1)S(1)}, u32[]{:S(2)}, u32[]{:S(2)}) %all-to-all-start.7) | async-done | bytes 262176 | tf_op jit(solution)/shard_map/all_to_all | solution.py:130
  172.4 4.7 %all-to-all-start.5 = ((bf16[8,128,512]{2,1,0:T(8,128)(2,1)}), bf16[8,128,512]{2,1,0:T(8,128)(2,1)S(1)}, u32[]{:S(2)}, u32[]{:S(2)}) async-start(bf16[8,128,512]{2,1,0:T(8,128)(2,1)} %copy.54), calls=%async_computation.5 | async-start | bytes 2097152 | tf_op jit(solution)/shard_map/all_to_all | solution.py:121
  177.1 0.1 copy.47
  177.2 0.8 copy.50
  178.1 0.1 copy.48
  178.2 0.8 copy.51
  179.0 24.4 %all-to-all-done.5 = bf16[8,128,512]{2,1,0:T(8,128)(2,1)S(1)} async-done(((bf16[8,128,512]{2,1,0:T(8,128)(2,1)}), bf16[8,128,512]{2,1,0:T(8,128)(2,1)S(1)}, u32[]{:S(2)}, u32[]{:S(2)}) %all-to-all-start.5) | async-done | bytes 1048608 | tf_op jit(solution)/shard_map/all_to_all | solution.py:121
  203.3 0.7 copy.46
  204.0 1.3 copy.49
  (32 shorter events, 0.4 us)
Async XLA Ops:
  0.6 0.9 copy-start
  2.3 16.2 %all-to-all-start = ((bf16[128,8,128]{2,0,1:T(8,128)(2,1)}), bf16[128,8,128]{2,0,1:T(8,128)(2,1)S(1)}, u32[]{:S(2)}, u32[]{:S(2)}) async-start(bf16[128,8,128]{2,0,1:T(8,128)(2,1)} %bitcast), calls=%async_computation | async-start | bytes 524288 | tf_op jit(solution)/shard_map/all_to_all | solution.py:45
  19.3 12.4 %all-to-all-start.2 = ((bf16[128,8,128]{2,0,1:T(8,128)(2,1)}), bf16[128,8,128]{2,0,1:T(8,128)(2,1)}, u32[]{:S(2)}, u32[]{:S(2)}) async-start(bf16[128,8,128]{2,0,1:T(8,128)(2,1)} %bitcast.5), calls=%async_computation.2 | async-start | bytes 524288 | tf_op jit(solution)/shard_map/all_to_all | solution.py:46
  31.7 29.0 %all-to-all-start.1 = ((bf16[128,8,512]{0,2,1:T(8,128)(2,1)}), bf16[128,8,512]{0,2,1:T(8,128)(2,1)S(1)}, u32[]{:S(2)}, u32[]{:S(2)}) async-start(bf16[128,8,512]{0,2,1:T(8,128)(2,1)} %bitcast.3), calls=%async_computation.1 | async-start | bytes 2097152 | tf_op jit(solution)/shard_map/all_to_all | solution.py:34
  60.7 29.6 %all-to-all-start.3 = ((bf16[128,8,512]{0,2,1:T(8,128)(2,1)}), bf16[128,8,512]{0,2,1:T(8,128)(2,1)}, u32[]{:S(2)}, u32[]{:S(2)}) async-start(bf16[128,8,512]{0,2,1:T(8,128)(2,1)} %bitcast.8), calls=%async_computation.3 | async-start | bytes 2097152 | tf_op jit(solution)/shard_map/all_to_all | solution.py:35
  64.9 12.5 %collective-permute-start.1 = (bf16[1024,128]{1,0:T(8,128)(2,1)}, bf16[1024,128]{1,0:T(8,128)(2,1)}, u32[]{:S(2)}, u32[]{:S(2)}) collective-permute-start(bf16[1024,128]{1,0:T(8,128)(2,1)} %bitcast.7), channel_id=1, source_target_pairs={{0,8},{8,16},{16,24},{1,9},{9,17},{17,25},{2,10},{10,18},{18,26},{... | collective-permute-start | bytes 786440 | tf_op jit(solution)/shard_map/ppermute | solution.py:15
  67.0 26.7 %collective-permute-start = (bf16[1024,128]{1,0:T(8,128)(2,1)S(1)}, bf16[1024,128]{1,0:T(8,128)(2,1)}, u32[]{:S(2)}, u32[]{:S(2)}) collective-permute-start(bf16[1024,128]{1,0:T(8,128)(2,1)S(1)} %bitcast.139), channel_id=1, source_target_pairs={{0,8},{8,16},{16,24},{1,9},{9,17},{17,25},{2,10},{10,18},{18,26},{... | collective-permute-start | bytes 786440 | tf_op jit(solution)/shard_map/ppermute | solution.py:15
  90.3 9.9 %all-to-all-start.4 = ((f32[128,8,4]{0,2,1:T(4,128)}), f32[128,8,4]{0,2,1:T(4,128)S(1)}, u32[]{:S(2)}, u32[]{:S(2)}) async-start(f32[128,8,4]{0,2,1:T(4,128)} %bitcast.10), calls=%async_computation.4 | async-start | bytes 32768 | tf_op jit(solution)/shard_map/all_to_all | solution.py:37
  104.0 5.5 %copy-start.1 = (f32[2048,128]{1,0:T(8,128)S(1)}, f32[2048,128]{1,0:T(8,128)}, u32[]{:S(2)}) copy-start(f32[2048,128]{1,0:T(8,128)} %get-tuple-element.368) | copy-start | bytes 3145732 | tf_op jit(solution)/shard_map/while
  104.0 5.5 %copy-start.3 = (bf16[1024,4,128]{0,2,1:T(8,128)(2,1)S(1)}, bf16[1024,4,128]{0,2,1:T(8,128)(2,1)}, u32[]{:S(2)}) copy-start(bf16[1024,4,128]{0,2,1:T(8,128)(2,1)} %get-tuple-element.388) | copy-start | bytes 3145732 | tf_op jit(solution)/shard_map/while
  109.5 4.1 %copy-start.4 = (bf16[2048,128]{1,0:T(8,128)(2,1)S(1)}, bf16[2048,128]{1,0:T(8,128)(2,1)}, u32[]{:S(2)}) copy-start(bf16[2048,128]{1,0:T(8,128)(2,1)} %get-tuple-element.387) | copy-start | bytes 1572868 | tf_op jit(solution)/shard_map/while
  113.6 8.7 %copy-start.2 = (f32[2048,128]{1,0:T(8,128)}, f32[2048,128]{1,0:T(8,128)S(1)}, u32[]{:S(2)}) copy-start(f32[2048,128]{1,0:T(8,128)S(1)} %fusion.78) | copy-start | bytes 3145732 | tf_op jit(solution)/shard_map/while
  123.8 5.6 %copy-start.1 = (f32[2048,128]{1,0:T(8,128)S(1)}, f32[2048,128]{1,0:T(8,128)}, u32[]{:S(2)}) copy-start(f32[2048,128]{1,0:T(8,128)} %get-tuple-element.368) | copy-start | bytes 3145732 | tf_op jit(solution)/shard_map/while
  123.8 5.6 %copy-start.3 = (bf16[1024,4,128]{0,2,1:T(8,128)(2,1)S(1)}, bf16[1024,4,128]{0,2,1:T(8,128)(2,1)}, u32[]{:S(2)}) copy-start(bf16[1024,4,128]{0,2,1:T(8,128)(2,1)} %get-tuple-element.388) | copy-start | bytes 3145732 | tf_op jit(solution)/shard_map/while
  129.4 4.1 %copy-start.4 = (bf16[2048,128]{1,0:T(8,128)(2,1)S(1)}, bf16[2048,128]{1,0:T(8,128)(2,1)}, u32[]{:S(2)}) copy-start(bf16[2048,128]{1,0:T(8,128)(2,1)} %get-tuple-element.387) | copy-start | bytes 1572868 | tf_op jit(solution)/shard_map/while
  133.5 8.8 %copy-start.2 = (f32[2048,128]{1,0:T(8,128)}, f32[2048,128]{1,0:T(8,128)S(1)}, u32[]{:S(2)}) copy-start(f32[2048,128]{1,0:T(8,128)S(1)} %fusion.78) | copy-start | bytes 3145732 | tf_op jit(solution)/shard_map/while
  142.3 3.7 %collective-permute-start.2 = (bf16[1024,128]{1,0:T(8,128)(2,1)S(1)}, bf16[1024,128]{1,0:T(8,128)(2,1)S(1)}, u32[]{:S(2)}, u32[]{:S(2)}) collective-permute-start(bf16[1024,128]{1,0:T(8,128)(2,1)S(1)} %slice.25), channel_id=1, source_target_pairs={{8,0},{16,8},{24,16},{9,1},{17,9},{25,17},{10,2},{18,10},{26,18},{... | collective-permute-start | bytes 786440 | tf_op jit(solution)/shard_map/ppermute | solution.py:15
  144.6 6.9 %collective-permute-start.3 = (bf16[1024,128]{1,0:T(8,128)(2,1)S(1)}, bf16[1024,128]{1,0:T(8,128)(2,1)S(1)}, u32[]{:S(2)}, u32[]{:S(2)}) collective-permute-start(bf16[1024,128]{1,0:T(8,128)(2,1)S(1)} %slice.24), channel_id=1, source_target_pairs={{8,0},{16,8},{24,16},{9,1},{17,9},{25,17},{10,2},{18,10},{26,18},{... | collective-permute-start | bytes 786440 | tf_op jit(solution)/shard_map/ppermute | solution.py:15
  146.7 13.0 %all-to-all-start.6 = ((bf16[8,128,128]{2,1,0:T(8,128)(2,1)}), bf16[8,128,128]{2,1,0:T(8,128)(2,1)S(1)}, u32[]{:S(2)}, u32[]{:S(2)}) async-start(bf16[8,128,128]{2,1,0:T(8,128)(2,1)} %bitcast.15), calls=%async_computation.6 | async-start | bytes 524288 | tf_op jit(solution)/shard_map/all_to_all | solution.py:123
  159.7 12.7 %all-to-all-start.7 = ((bf16[8,128,128]{2,1,0:T(8,128)(2,1)}), bf16[8,128,128]{2,1,0:T(8,128)(2,1)S(1)}, u32[]{:S(2)}, u32[]{:S(2)}) async-start(bf16[8,128,128]{2,1,0:T(8,128)(2,1)} %bitcast.19), calls=%async_computation.7 | async-start | bytes 524288 | tf_op jit(solution)/shard_map/all_to_all | solution.py:130
  172.4 30.9 %all-to-all-start.5 = ((bf16[8,128,512]{2,1,0:T(8,128)(2,1)}), bf16[8,128,512]{2,1,0:T(8,128)(2,1)S(1)}, u32[]{:S(2)}, u32[]{:S(2)}) async-start(bf16[8,128,512]{2,1,0:T(8,128)(2,1)} %copy.54), calls=%async_computation.5 | async-start | bytes 2097152 | tf_op jit(solution)/shard_map/all_to_all | solution.py:121
where the time goes:
time: 207 us; the launch traced here: 205 us
  waiting for transfers between devices  86.2 us (42%)
  starting transfers between devices  44.5 us (21%)
  matrix products  30.4 us (15%)
  local copies, waits for them, and re-layouts  24.7 us (12%)
  other arithmetic  18.6 us (9%)
    all_to_all x1, waiting for transfers between devices, local(): lax.all_to_all(query_low, 'uly', split_axis=0, concat_axis=1, tiled=True)  24.4 us
    all_to_all x1, waiting for transfers between devices, local(): lax.all_to_all(query, 'uly', split_axis=1, concat_axis=0, tiled=True)  23.2 us
    unnamed x9, local copies, waits for them, and re-layouts  11.5 us
    all_to_all x1, waiting for transfers between devices, local(): lax.all_to_all(out_grad, 'uly', split_axis=1, concat_axis=0, tiled=True)  11 us
    dot_general x2, matrix products, block_step(): jnp.einsum('qhd,kd->hqk', grad_block, value_block, preferred_element_type...  10.2 us
    ppermute x4, starting transfers between devices, shifted(): lax.ppermute(value, axis, [(source, source + steps) for source in range(l...  8.71 us
    dot_general x2, matrix products, block_step(): jnp.einsum('hqk,qhd->kd', weights_low, grad_block, preferred_element_type...  8.17 us
    all_to_all x1, waiting for transfers between devices, local(): lax.all_to_all(repeat_groups(key_input), 'uly', split_axis=1, concat_axis...  7.99 us
  transfers between devices with their start and end apart: 12, of which 8 were waited for; matrix products, arithmetic and copies ran while one was open for 13% of the time, Pallas kernels for 0%

commit v1 on v0

v1 whole, which is shorter than its diff:
```python
import functools
import math

import jax
import jax.numpy as jnp
from jax import lax
from jax.experimental import pallas as pl
from jax.experimental.pallas import tpu as pltpu
from jax.sharding import PartitionSpec as P

QUERY_HEADS = 32
KEY_VALUE_HEADS = 4
HEAD_SIZE = 128
WINDOW_KEYS = 1024
GROUP = QUERY_HEADS // KEY_VALUE_HEADS
PAIRS = GROUP // 2
MESH = pl.DeviceIdType.MESH
F32 = jnp.float32
BF16 = jnp.bfloat16
NT = (((1,), (1,)), ((), ()))
TN = (((0,), (0,)), ((), ()))


def kernel(
    rows, back, blks, ulys,
    q_hbm, k_hbm, v_hbm, o_hbm, g_hbm,
    dq_ref, dk_ref, dv_ref,
    q_ref, o_ref, g_ref, kv, acc_k, acc_v, own, pg_send, pg_recv, c_send, c_recv,
    load_sem, kv_sem, chain_ss, chain_rs, pair_ss, pair_rs, pgs, pgr, cgs, cgr,
):
    half = back // 2
    heads = KEY_VALUE_HEADS
    scaling = HEAD_SIZE ** (-0.5)
    total = blks * ulys
    me = lax.axis_index("blk") * ulys + lax.axis_index("uly")
    par = lax.rem(me, 2)
    partner = me + 1 - 2 * par
    up, down = me + 2, me - 2
    has_up, has_down = up < total, down >= 0

    def where_is(t):
        return (t // ulys, lax.rem(t, ulys))

    loads = [
        pltpu.make_async_copy(s, d, load_sem.at[i])
        for i, (s, d) in enumerate(((q_hbm, q_ref), (o_hbm, o_ref), (g_hbm, g_ref)))
    ]
    kv_loads = []
    for h in range(heads):
        for i, src in enumerate((k_hbm, v_hbm)):
            kv_loads.append(
                pltpu.make_async_copy(
                    src.at[:, h * HEAD_SIZE : (h + 1) * HEAD_SIZE], kv.at[h, back, i], kv_sem.at[h, i]
                )
            )
    for copy in kv_loads:
        copy.start()
    for copy in loads:
        copy.start()

    barrier = pltpu.get_barrier_semaphore()

    @pl.when(has_up)
    def _():
        pl.semaphore_signal(barrier, inc=1, device_id=where_is(up), device_id_type=MESH)

    @pl.when(has_down)
    def _():
        pl.semaphore_signal(barrier, inc=1, device_id=where_is(down), device_id_type=MESH)

    pl.semaphore_signal(barrier, inc=1, device_id=where_is(partner), device_id_type=MESH)
    pl.semaphore_wait(barrier, 1 + has_up.astype(jnp.int32) + has_down.astype(jnp.int32))

    def clear(s, carry):
        @pl.when(me - back + s < 0)
        def _():
            for h in range(heads):
                kv[h, s] = jnp.zeros((2, rows, HEAD_SIZE), BF16)

        return carry

    lax.fori_loop(0, back, clear, 0)

    def chain_copy(h, k):
        return pltpu.make_async_remote_copy(
            src_ref=kv.at[h, back - 2 * k],
            dst_ref=kv.at[h, back - 2 * k - 2],
            send_sem=chain_ss.at[h, k],
            recv_sem=chain_rs.at[h, k],
            device_id=where_is(up),
            device_id_type=MESH,
        )

    def pair_copy(h, k):
        return pltpu.make_async_remote_copy(
            src_ref=kv.at[h, back - 2 * k - 2 * par],
            dst_ref=kv.at[h, back - 1 - 2 * k],
            send_sem=pair_ss.at[h, k],
            recv_sem=pair_rs.at[h, k],
            device_id=where_is(partner),
            device_id_type=MESH,
        )

    def chain_out(k):
        return has_up & (me - 2 * k >= 0)

    def pair_out(k):
        return me - 2 * k - 2 * par >= 0

    def send_own(h):
        @pl.when(has_up)
        def _():
            chain_copy(h, 0).start()

        @pl.when(par == 0)
        def _():
            pair_copy(h, 0).start()

    def gather_step(h, k):
        @pl.when(me - 2 * k - 2 >= 0)
        def _():
            chain_copy(h, k).wait_recv()

            @pl.when(has_up & (k < half - 1))
            def _():
                chain_copy(h, k + 1).start()

            nxt = k + 1 - par

            @pl.when(nxt < half)
            def _():
                pair_copy(h, nxt).start()

    def gather_finish(h, k):
        @pl.when(me - 1 - 2 * k >= 0)
        def _():
            pair_copy(h, k).wait_recv()

    def pg_copy(h, k):
        return pltpu.make_async_remote_copy(
            src_ref=pg_send.at[h, k],
            dst_ref=pg_recv.at[h, k],
            send_sem=pgs.at[h, k],
            recv_sem=pgr.at[h, k],
            device_id=where_is(partner),
            device_id_type=MESH,
        )

    def cg_copy(h, j):
        return pltpu.make_async_remote_copy(
            src_ref=c_send.at[h, j],
            dst_ref=c_recv.at[h, j],
            send_sem=cgs.at[h, j],
            recv_sem=cgr.at[h, j],
            device_id=where_is(down),
            device_id_type=MESH,
        )

    def pg_out(h, k):
        s = back - 1 - 2 * k
        at = pl.ds(s * rows, rows)
        pg_send[h, k, 0] = (acc_k[at, :] * scaling).astype(BF16)
        pg_send[h, k, 1] = acc_v[at, :].astype(BF16)

        @pl.when(me - 1 - 2 * k >= 0)
        def _():
            pg_copy(h, k).start()

    def keep_own(h, e):
        at = pl.ds((back - 2 * e) * rows, rows)
        own[h, e, 0] = acc_k[at, :] * scaling
        own[h, e, 1] = acc_v[at, :]

    def reduce_step(h, j):
        e = half - j

        @pl.when(me - 2 * e >= 0)
        def _():
            k = e - par

            @pl.when((k >= 0) & (k < half))
            def _():
                pg_copy(h, k).wait_recv()
                own[h, e] = own[h, e] + pg_recv[h, k].astype(F32)

            @pl.when(has_up & (j > 0))
            def _():
                cg_copy(h, j - 1).wait_recv()
                own[h, e] = own[h, e] + c_recv[h, j - 1].astype(F32)

    def reduce_send(h, j):
        @pl.when(me - 2 * (half - j) >= 0)
        def _():
            c_send[h, j] = own[h, half - j].astype(BF16)
            cg_copy(h, j).start()

    def finish(h):
        reduce_step(h, half)
        columns = pl.ds(pl.multiple_of(h * HEAD_SIZE, HEAD_SIZE), HEAD_SIZE)
        dk_ref[:, columns] = own[h, 0, 0].astype(BF16)
        dv_ref[:, columns] = own[h, 0, 1].astype(BF16)

    def compute(h, p):
        first = pl.multiple_of((h * GROUP + 2 * p) * HEAD_SIZE, HEAD_SIZE)
        second = pl.multiple_of(first + HEAD_SIZE, HEAD_SIZE)

        def two(ref):
            return jnp.concatenate(
                [ref[:, pl.ds(first, HEAD_SIZE)], ref[:, pl.ds(second, HEAD_SIZE)]], axis=0
            )

        q2, g2, o2 = two(q_ref), two(g_ref), two(o_ref)
        rd = jnp.sum((o2.astype(F32) * g2.astype(F32)).T, axis=0, keepdims=True)
        keys = kv[h, :, 0].reshape((back + 1) * rows, HEAD_SIZE)
        values = kv[h, :, 1].reshape((back + 1) * rows, HEAD_SIZE)
        st = lax.dot_general(keys, q2, NT, preferred_element_type=F32)
        dp = lax.dot_general(values, g2, NT, preferred_element_type=F32)
        key_at = lax.broadcasted_iota(jnp.int32, (rows, 2 * rows), 0)
        query_at = lax.rem(lax.broadcasted_iota(jnp.int32, (rows, 2 * rows), 1), rows)
        tri = key_at > query_at
        gone = [jnp.where(me - back + s < 0, 1e30, 0.0).astype(F32) for s in range(back)]

        def cut(a, s):
            return a[s * rows : (s + 1) * rows]

        c = scaling * math.log2(math.e)
        blocks = [jnp.where(tri, cut(st, 0) - gone[0], cut(st, back))]
        blocks += [cut(st, s) for s in range(1, back)]
        top = jnp.max(blocks[0], axis=0, keepdims=True)
        for s in range(1, back):
            top = jnp.maximum(top, jnp.max(blocks[s], axis=0, keepdims=True) - gone[s])
        top = top * c
        probs = [jnp.exp2(blocks[0] * c - top)]
        probs += [jnp.exp2(blocks[s] * c - (top + gone[s])) for s in range(1, back)]
        sums = jnp.sum(probs[0], axis=0, keepdims=True)
        for s in range(1, back):
            sums = sums + jnp.sum(probs[s], axis=0, keepdims=True)
        inv = 1.0 / sums
        dps = [jnp.where(tri, cut(dp, 0), cut(dp, back))] + [cut(dp, s) for s in range(1, back)]
        ws = [a * inv for a in probs]
        ds = [w * (a - rd) for w, a in zip(ws, dps)]

        def spread(parts):
            low = [jnp.where(tri, parts[0], 0.0)] + parts[1:] + [jnp.where(tri, 0.0, parts[0])]
            return jnp.concatenate([a.astype(BF16) for a in low], axis=0)

        wt, dst = spread(ws), spread(ds)
        acc_v[...] += jnp.dot(wt, g2, preferred_element_type=F32)
        acc_k[...] += jnp.dot(dst, q2, preferred_element_type=F32)
        dq = lax.dot_general(dst, keys, TN, preferred_element_type=F32) * scaling
        dq_ref[:, pl.ds(first, HEAD_SIZE)] = dq[:rows].astype(BF16)
        dq_ref[:, pl.ds(second, HEAD_SIZE)] = dq[rows:].astype(BF16)

    for h in range(heads):
        kv_loads[2 * h].wait()
        kv_loads[2 * h + 1].wait()
        send_own(h)

    def loop(count, fn):
        def body(i, carry):
            fn(i)
            return carry

        lax.fori_loop(0, count, body, 0)

    loop(half, lambda k: gather_step(0, k))
    for copy in loads:
        copy.wait()

    def per_head(h):
        loop(half, lambda k: gather_finish(h, k))
        acc_k[...] = jnp.zeros_like(acc_k)
        acc_v[...] = jnp.zeros_like(acc_v)

        def part(p):
            compute(h, p)

            @pl.when((h + 1 < heads) & (p < half))
            def _():
                gather_step(h + 1, p)

            @pl.when((h > 0) & (p < half))
            def _():
                reduce_step(h - 1, p)
                reduce_send(h - 1, p)

        loop(PAIRS, part)

        def rest(k):
            @pl.when(h + 1 < heads)
            def _():
                gather_step(h + 1, k)

            @pl.when(h > 0)
            def _():
                reduce_step(h - 1, k)
                reduce_send(h - 1, k)

        for k in range(PAIRS, half):
            rest(k)
        loop(half, lambda k: pg_out(h, k))
        loop(half + 1, lambda e: keep_own(h, e))

        @pl.when(h > 0)
        def _():
            finish(h - 1)

    loop(heads, per_head)

    def last(j):
        reduce_step(heads - 1, j)
        reduce_send(heads - 1, j)

    loop(half, last)
    finish(heads - 1)

    def drain(h):
        def inner(k):
            @pl.when(chain_out(k))
            def _():
                chain_copy(h, k).wait_send()

            @pl.when(pair_out(k))
            def _():
                pair_copy(h, k).wait_send()

            @pl.when(me - 1 - 2 * k >= 0)
            def _():
                pg_copy(h, k).wait_send()

            @pl.when(me - 2 * (half - k) >= 0)
            def _():
                cg_copy(h, k).wait_send()

        loop(half, inner)

    loop(heads, drain)


def local(query, key_input, value_input, output, out_grad):
    rows, width = query.shape
    blks, ulys = lax.axis_size("blk"), lax.axis_size("uly")
    back = WINDOW_KEYS // rows
    half = back // 2
    heads = KEY_VALUE_HEADS
    span = (back + 1) * rows
    pair = (2, rows, HEAD_SIZE)
    dma = pltpu.SemaphoreType.DMA
    any_spec = pl.BlockSpec(memory_space=pl.ANY)
    vmem_spec = pl.BlockSpec(memory_space=pltpu.VMEM)
    return pl.pallas_call(
        functools.partial(kernel, rows, back, blks, ulys),
        out_shape=(
            jax.ShapeDtypeStruct(query.shape, BF16),
            jax.ShapeDtypeStruct(key_input.shape, BF16),
            jax.ShapeDtypeStruct(value_input.shape, BF16),
        ),
        in_specs=[any_spec] * 5,
        out_specs=(vmem_spec,) * 3,
        scratch_shapes=[
            pltpu.VMEM((rows, width), BF16),
            pltpu.VMEM((rows, width), BF16),
            pltpu.VMEM((rows, width), BF16),
            pltpu.VMEM((heads, back + 1) + pair, BF16),
            pltpu.VMEM((span, HEAD_SIZE), F32),
            pltpu.VMEM((span, HEAD_SIZE), F32),
            pltpu.VMEM((heads, half + 1) + pair, F32),
            pltpu.VMEM((heads, half) + pair, BF16),
            pltpu.VMEM((heads, half) + pair, BF16),
            pltpu.VMEM((heads, half) + pair, BF16),
            pltpu.VMEM((heads, half) + pair, BF16),
            dma((3,)),
            dma((heads, 2)),
        ]
        + [dma((heads, half))] * 8,
        compiler_params=pltpu.CompilerParams(
            collective_id=0, has_side_effects=True, vmem_limit_bytes=60 * 1024 * 1024
        ),
    )(query, key_input, value_input, output, out_grad)


def solution(mesh):
    spec = P(("blk", "uly"), None)
    return jax.shard_map(
        local, mesh=mesh, in_specs=(spec,) * 5, out_specs=(spec,) * 3, check_vma=False
    )
```

time: 207 us -> 111 us (0.54)
  Pallas kernels: 0 us -> 104 us
  waiting for transfers between devices: 86.2 us -> 0 us
  starting transfers between devices: 44.5 us -> 0 us
  matrix products: 30.4 us -> 0 us
  local copies, waits for them, and re-layouts: 24.7 us -> 3.93 us
  other arithmetic: 18.6 us -> 0 us
    pallas_call x0 -> x1, Pallas kernels: none -> 104 us  [local(): pl.pallas_call(functools.partial(kernel, rows, back, blks, ulys), out_sha...]
    all_to_all x8 -> x0, waiting for transfers between devices: 86.2 us -> none  [the longest x1 24.4 us: local(): lax.all_to_all(query_low, 'uly', split_axis=0, concat_axis=1, tiled=True)]
    all_to_all x8 -> x0, starting transfers between devices: 35.7 us -> none  [the longest x1 7.31 us: local(): lax.all_to_all(repeat_groups(key_input), 'uly', split_axis=1, concat_axis...]
    dot_general x10 -> x0, matrix products: 30.4 us -> none  [the longest x2 10.2 us: block_step(): jnp.einsum('qhd,kd->hqk', grad_block, value_block, preferred_element_type...]
    ppermute x4 -> x0, starting transfers between devices: 8.71 us -> none  [shifted(): lax.ppermute(value, axis, [(source, source + steps) for source in range(l...]
    reduce_sum x5 -> x0, other arithmetic: 8.55 us -> none  [the longest x2 6.27 us: block_step(): jnp.sum(jnp.where(visible, jnp.exp(masked - row_max[:, :, None]), 0.0), a...]
    unnamed x9 -> x7, local copies, waits for them, and re-layouts: 11.5 us -> 3.93 us
    all_to_all x4 -> x0, local copies, waits for them, and re-layouts: 4.7 us -> none  [the longest x2 2.11 us: local(): lax.all_to_all(query_low, 'uly', split_axis=0, concat_axis=1, tiled=True)]
  transfers between devices with their start and end apart: 12 -> 0, of which waited for: 8 -> 0; matrix products, arithmetic and copies ran while one was open for 13% -> 0% of each run, Pallas kernels for 0% -> 0%
where the time goes in v1:
time: 111 us; the launch traced here: 109 us
  Pallas kernels  104 us (94%)
  local copies, waits for them, and re-layouts  3.93 us (4%)
    pallas_call x1, Pallas kernels, local(): pl.pallas_call(functools.partial(kernel, rows, back, blks, ulys), out_sha...  104 us
    unnamed x7, local copies, waits for them, and re-layouts  3.93 us

profile of v1, /device:TPU:0, one launch (start us, length us, event | category | flops | bytes accessed | tf_op | source)
XLA Modules:
  0.0 108.8 jit_solution(2980391280914794015)
XLA Ops:
  0.6 104.2 %shard_map.76 = (bf16[128,4096]{1,0:T(8,128)(2,1)}, bf16[128,512]{1,0:T(8,128)(2,1)}, bf16[128,512]{1,0:T(8,128)(2,1)}) custom-call(bf16[128,4096]{1,0:T(8,128)(2,1)} %q_hbm.1, bf16[128,512]{1,0:T(8,128)(2,1)} %k_hbm.1, bf16[128,512]{1,0:T(8,128)(2,1)} %v_hbm.1, bf16[128,4096]{1,0:T(8,128)(2,1)} %o_hbm.1, bf16[128,4096]{1,0:T(8,128)(2,1)} %g_hbm.1), custom_call_target="tpu_custom_call" | custom-call | tf_op jit(solution)/shard_map/pallas_call | solution.py:351
  104.9 0.0 copy-start.1
  104.9 2.3 %copy.11 = bf16[128,4096]{1,0:T(8,128)(2,1)} copy(bf16[128,4096]{1,0:T(8,128)(2,1)} %get-tuple-element.6) | data formatting | bytes 2097152
  107.2 0.0 copy-done.1
  107.2 0.0 copy-start
  107.2 0.7 copy.12
  107.9 0.3 copy-done
  108.2 0.7 copy.13
Async XLA Ops:
  104.9 2.3 %copy-start.1 = (bf16[128,512]{1,0:T(8,128)(2,1)S(1)}, bf16[128,512]{1,0:T(8,128)(2,1)}, u32[]{:S(2)}) copy-start(bf16[128,512]{1,0:T(8,128)(2,1)} %get-tuple-element.7) | copy-start | bytes 393220
  107.2 1.0 copy-start

commit v2 on v1

--- a/solution.py
+++ b/solution.py
@@ -263,56 +263,60 @@
 
         lax.fori_loop(0, count, body, 0)
 
-    loop(half, lambda k: gather_step(0, k))
+    def hop(k):
+        loop(heads, lambda h: gather_step(h, k))
+
+    loop(half - 1, hop)
+    gather_step(0, half - 1)
     for copy in loads:
         copy.wait()
 
+    def job(h, j):
+        @pl.when((h >= 0) & (h < heads) & (j < half))
+        def _():
+            reduce_step(h, j)
+            reduce_send(h, j)
+
+        @pl.when((h >= 0) & (h < heads) & (j == half))
+        def _():
+            finish(h)
+
+    lag = half + 1
+
     def per_head(h):
-        loop(half, lambda k: gather_finish(h, k))
-        acc_k[...] = jnp.zeros_like(acc_k)
-        acc_v[...] = jnp.zeros_like(acc_v)
-
-        def part(p):
-            compute(h, p)
-
-            @pl.when((h + 1 < heads) & (p < half))
-            def _():
-                gather_step(h + 1, p)
-
-            @pl.when((h > 0) & (p < half))
-            def _():
-                reduce_step(h - 1, p)
-                reduce_send(h - 1, p)
-
-        loop(PAIRS, part)
-
-        def rest(k):
-            @pl.when(h + 1 < heads)
-            def _():
-                gather_step(h + 1, k)
-
-            @pl.when(h > 0)
-            def _():
-                reduce_step(h - 1, k)
-                reduce_send(h - 1, k)
-
-        for k in range(PAIRS, half):
-            rest(k)
-        loop(half, lambda k: pg_out(h, k))
-        loop(half + 1, lambda e: keep_own(h, e))
-
-        @pl.when(h > 0)
-        def _():
-            finish(h - 1)
-
-    loop(heads, per_head)
-
-    def last(j):
-        reduce_step(heads - 1, j)
-        reduce_send(heads - 1, j)
-
-    loop(half, last)
-    finish(heads - 1)
+        @pl.when(h < heads)
+        def _():
+            loop(half, lambda k: gather_finish(h, k))
+            acc_k[...] = jnp.zeros_like(acc_k)
+            acc_v[...] = jnp.zeros_like(acc_v)
+
+        def part(i):
+            p = 2 * i
+
+            @pl.when(h < heads)
+            def _():
+                compute(h, p)
+                compute(h, p + 1)
+
+            @pl.when((h == 0) & (p + 1 < heads))
+            def _():
+                gather_step(p + 1, half - 1)
+
+            @pl.when((h == 0) & (p + 2 < heads))
+            def _():
+                gather_step(p + 2, half - 1)
+
+        loop(PAIRS // 2, part)
+
+        @pl.when(h < heads)
+        def _():
+            loop(half, lambda k: pg_out(h, k))
+            loop(half + 1, lambda e: keep_own(h, e))
+
+        for m in range(1, lag + 1):
+            job(h - m, m - 1)
+
+    loop(heads + lag, per_head)
 
     def drain(h):
         def inner(k):

time: 111 us -> 81.1 us (0.73)
  the two profiles are of different devices: /device:TPU:0 before, /device:TPU:29 now
where the time goes in v2:
time: 81.1 us; the launch traced here: 80.9 us
  Pallas kernels  76.3 us (94%)
  local copies, waits for them, and re-layouts  3.93 us (5%)
    pallas_call x1, Pallas kernels, local(): pl.pallas_call(functools.partial(kernel, rows, back, blks, ulys), out_sha...  76.3 us
    unnamed x7, local copies, waits for them, and re-layouts  3.93 us

profile of v2, /device:TPU:29, one launch (start us, length us, event | category | flops | bytes accessed | tf_op | source)
XLA Modules:
  0.0 80.9 jit_solution(15494828834606426264)
XLA Ops:
  0.6 76.3 %shard_map.76 = (bf16[128,4096]{1,0:T(8,128)(2,1)}, bf16[128,512]{1,0:T(8,128)(2,1)}, bf16[128,512]{1,0:T(8,128)(2,1)}) custom-call(bf16[128,4096]{1,0:T(8,128)(2,1)} %q_hbm.1, bf16[128,512]{1,0:T(8,128)(2,1)} %k_hbm.1, bf16[128,512]{1,0:T(8,128)(2,1)} %v_hbm.1, bf16[128,4096]{1,0:T(8,128)(2,1)} %o_hbm.1, bf16[128,4096]{1,0:T(8,128)(2,1)} %g_hbm.1), custom_call_target="tpu_custom_call" | custom-call | tf_op jit(solution)/shard_map/pallas_call | solution.py:355
  77.0 0.0 copy-start.1
  77.0 2.3 %copy.11 = bf16[128,4096]{1,0:T(8,128)(2,1)} copy(bf16[128,4096]{1,0:T(8,128)(2,1)} %get-tuple-element.6) | data formatting | bytes 2097152
  79.3 0.0 copy-done.1
  79.3 0.0 copy-start
  79.3 0.7 copy.12
  80.0 0.3 copy-done
  80.3 0.7 copy.13
Async XLA Ops:
  77.0 2.3 %copy-start.1 = (bf16[128,512]{1,0:T(8,128)(2,1)S(1)}, bf16[128,512]{1,0:T(8,128)(2,1)}, u32[]{:S(2)}) copy-start(bf16[128,512]{1,0:T(8,128)(2,1)} %get-tuple-element.7) | copy-start | bytes 393220
  79.3 1.0 %copy-start = (bf16[128,512]{1,0:T(8,128)(2,1)S(1)}, bf16[128,512]{1,0:T(8,128)(2,1)}, u32[]{:S(2)}) copy-start(bf16[128,512]{1,0:T(8,128)(2,1)} %get-tuple-element.8) | copy-start | bytes 393220
